TPU v7x, 8 devices: a whole 2x2x1 slice. The times are simulated.
8 devices in a mesh: tp: 2 (over z, y), ep: 4 (over x, core).
Axes of the slice: x: 2, y: 2, z: 1, core: 2. Of those that a mesh axis runs over, the one named last changes fastest.
Arguments:
- x: bfloat16 [1536, 1536], P(('ep', 'tp'))
- grad_y: bfloat16 [1536, 1536], P(('ep', 'tp'))
- w_router: bfloat16 [1536, 64], replicated
- w_gate: bfloat16 [64, 1536, 512], P('ep', None, 'tp')
- w_up: bfloat16 [64, 1536, 512], P('ep', None, 'tp')
- w_down: bfloat16 [64, 512, 1536], P('ep', 'tp')
- ws_gate: bfloat16 [1536, 1024], P(None, 'tp')
- ws_up: bfloat16 [1536, 1024], P(None, 'tp')
- ws_down: bfloat16 [1024, 1536], P('tp')
- topk_idx: int32 [1536, 6], P(('ep', 'tp'))
Outputs:
- output 1: bfloat16 [1536, 1536], P(('ep', 'tp'))
- output 2: bfloat16 [1536, 1536], P(('ep', 'tp'))
- output 3: float32 [1536, 64], replicated
- output 4: float32 [64, 1536, 512], P('ep', None, 'tp')
- output 5: float32 [64, 1536, 512], P('ep', None, 'tp')
- output 6: float32 [64, 512, 1536], P('ep', 'tp')
- output 7: float32 [1536, 1024], P(None, 'tp')
- output 8: float32 [1536, 1024], P(None, 'tp')
- output 9: float32 [1024, 1536], P('tp')
All inputs are finite; a program needn't handle non-finite values.
Results may differ from a plain program's by a relative error of at most 0.0131065.
Values are sent between devices in bfloat16 or wider.
A program may use at most 1 GiB of HBM per device.

v0:
```python
import jax
import jax.numpy as jnp
from jax import lax
from jax.sharding import PartitionSpec as P

GATE_SCALE = 16.0


def capacity(tok_rows, top_k, experts, ep_size):
    groups = top_k // 2
    most = groups * tok_rows // (2 * ep_size) + min(groups, ep_size // 2) * tok_rows // ep_size
    per_group = experts // ep_size
    return (2 * most + per_group - 1) // per_group


def slot_maps(topk_idx, route_gates, experts, capacity_rows):
    tok_rows = topk_idx.shape[0]
    n_slots = experts * capacity_rows
    hit_count = jnp.sum(jax.nn.one_hot(topk_idx, experts, dtype=jnp.int32), axis=1)
    slot_rank = jnp.cumsum(hit_count, axis=0) - hit_count
    slot_of = topk_idx * capacity_rows + jnp.take_along_axis(slot_rank, topk_idx, axis=1)
    flat_slot = slot_of.reshape(-1)
    token_ids = jnp.broadcast_to(jnp.arange(tok_rows, dtype=jnp.int32)[:, None], slot_of.shape).reshape(-1)
    slot_owner = jax.ops.segment_sum(token_ids - tok_rows, flat_slot, num_segments=n_slots) + tok_rows
    gate_slot = jax.ops.segment_sum(route_gates.reshape(-1), flat_slot, num_segments=n_slots)
    return slot_of, slot_owner, gate_slot


def swiglu_act(gate_pre, up_pre):
    return jax.nn.silu(gate_pre) * up_pre


def solution(mesh):
    tp_size = mesh.shape['tp']
    ep_size = mesh.shape['ep']

    def device_step(x, grad_y, w_router, w_gate, w_up, w_down, ws_gate, ws_up, ws_down, topk_idx):
        tok_rows, model_dim = x.shape
        top_k = topk_idx.shape[1]
        experts = w_router.shape[1]
        local_exp = w_gate.shape[0]
        capacity_rows = capacity(tok_rows, top_k, experts, ep_size)
        n_slots = experts * capacity_rows
        router_probs = jax.nn.softmax(jnp.dot(x, w_router, preferred_element_type=jnp.float32), axis=-1)
        route_gates = GATE_SCALE * jnp.take_along_axis(router_probs, topk_idx, axis=1)
        slot_of, slot_owner, gate_slot = slot_maps(topk_idx, route_gates, experts, capacity_rows)
        send_rows = jnp.take(x, slot_owner, axis=0, mode='fill', fill_value=0).reshape(ep_size, local_exp, capacity_rows, model_dim)
        recv_rows = lax.all_to_all(send_rows, 'ep', 0, 0)
        expert_rows = lax.all_gather(recv_rows, 'tp', axis=0)
        gate_pre = jnp.einsum('tsecd,edf->tsecf', expert_rows, w_gate, preferred_element_type=jnp.float32).astype(jnp.bfloat16)
        up_pre = jnp.einsum('tsecd,edf->tsecf', expert_rows, w_up, preferred_element_type=jnp.float32).astype(jnp.bfloat16)
        hidden_act = swiglu_act(gate_pre.astype(jnp.float32), up_pre.astype(jnp.float32)).astype(jnp.bfloat16)
        part_out = jnp.einsum('tsecf,efd->tsecd', hidden_act, w_down, preferred_element_type=jnp.float32)
        own_out = lax.psum_scatter(part_out, 'tp', scatter_dimension=0).astype(jnp.bfloat16)
        back_rows = lax.all_to_all(own_out, 'ep', 0, 0).reshape(n_slots, model_dim)
        picked = jnp.take(back_rows, slot_of, axis=0)
        routed = jnp.einsum('tk,tkd->td', route_gates, picked, preferred_element_type=jnp.float32)
        x_group = lax.all_gather(x, 'tp', axis=0, tiled=True)
        sg_pre = jnp.dot(x_group, ws_gate, preferred_element_type=jnp.float32).astype(jnp.bfloat16)
        su_pre = jnp.dot(x_group, ws_up, preferred_element_type=jnp.float32).astype(jnp.bfloat16)
        s_hidden = swiglu_act(sg_pre.astype(jnp.float32), su_pre.astype(jnp.float32)).astype(jnp.bfloat16)
        shared = lax.psum_scatter(jnp.dot(s_hidden, ws_down, preferred_element_type=jnp.float32), 'tp', scatter_dimension=0, tiled=True)
        y_out = (shared + routed).astype(jnp.bfloat16)

        d_gates = jnp.einsum('td,tkd->tk', grad_y, picked, preferred_element_type=jnp.float32)
        d_out = (jnp.take(grad_y, slot_owner, axis=0, mode='fill', fill_value=0) * gate_slot[:, None]).astype(jnp.bfloat16)
        d_recv = lax.all_to_all(d_out.reshape(ep_size, local_exp, capacity_rows, model_dim), 'ep', 0, 0)
        d_rows_in = lax.all_gather(d_recv, 'tp', axis=0)
        d_hidden = jnp.einsum('tsecd,efd->tsecf', d_rows_in, w_down, preferred_element_type=jnp.float32).astype(jnp.bfloat16)
        d_w_down = jnp.einsum('tsecf,tsecd->efd', hidden_act, d_rows_in, preferred_element_type=jnp.float32)
        act_out, act_vjp = jax.vjp(swiglu_act, gate_pre.astype(jnp.float32), up_pre.astype(jnp.float32))
        d_gate_pre, d_up_pre = act_vjp(d_hidden.astype(jnp.float32))
        d_gate_pre = d_gate_pre.astype(jnp.bfloat16)
        d_up_pre = d_up_pre.astype(jnp.bfloat16)
        d_w_gate = jnp.einsum('tsecd,tsecf->edf', expert_rows, d_gate_pre, preferred_element_type=jnp.float32)
        d_w_up = jnp.einsum('tsecd,tsecf->edf', expert_rows, d_up_pre, preferred_element_type=jnp.float32)
        d_rows_part = jnp.einsum('tsecf,edf->tsecd', d_gate_pre, w_gate, preferred_element_type=jnp.float32) + jnp.einsum('tsecf,edf->tsecd', d_up_pre, w_up, preferred_element_type=jnp.float32)
        d_own = lax.psum_scatter(d_rows_part, 'tp', scatter_dimension=0).astype(jnp.bfloat16)
        d_back = lax.all_to_all(d_own, 'ep', 0, 0).reshape(n_slots, model_dim)
        dx_routed = jnp.sum(jnp.take(d_back, slot_of, axis=0), axis=1, dtype=jnp.float32)
        d_scores = GATE_SCALE * jnp.einsum('tk,tke->te', d_gates, jax.nn.one_hot(topk_idx, experts, dtype=jnp.float32))
        d_logits = router_probs * (d_scores - jnp.sum(router_probs * d_scores, axis=-1, keepdims=True))
        d_router = lax.psum(jnp.einsum('td,te->de', x, d_logits, preferred_element_type=jnp.float32), ('tp', 'ep'))
        dx_router = jnp.einsum('te,de->td', d_logits, w_router, preferred_element_type=jnp.float32)
        dy_group = lax.all_gather(grad_y, 'tp', axis=0, tiled=True)
        ds_hidden = jnp.einsum('td,fd->tf', dy_group, ws_down, preferred_element_type=jnp.float32).astype(jnp.bfloat16)
        ds_down = lax.psum(jnp.einsum('tf,td->fd', s_hidden, dy_group, preferred_element_type=jnp.float32), 'ep')
        s_out, s_vjp = jax.vjp(swiglu_act, sg_pre.astype(jnp.float32), su_pre.astype(jnp.float32))
        dsg_pre, dsu_pre = s_vjp(ds_hidden.astype(jnp.float32))
        dsg_pre = dsg_pre.astype(jnp.bfloat16)
        dsu_pre = dsu_pre.astype(jnp.bfloat16)
        ds_gate = lax.psum(jnp.einsum('td,tf->df', x_group, dsg_pre, preferred_element_type=jnp.float32), 'ep')
        ds_up = lax.psum(jnp.einsum('td,tf->df', x_group, dsu_pre, preferred_element_type=jnp.float32), 'ep')
        dx_part = jnp.einsum('tf,df->td', dsg_pre, ws_gate, preferred_element_type=jnp.float32) + jnp.einsum('tf,df->td', dsu_pre, ws_up, preferred_element_type=jnp.float32)
        dx_shared = lax.psum_scatter(dx_part, 'tp', scatter_dimension=0, tiled=True)
        dx_out = (dx_router + dx_shared + dx_routed).astype(jnp.bfloat16)
        return y_out, dx_out, d_router, d_w_gate, d_w_up, d_w_down, ds_gate, ds_up, ds_down

    tok_spec = P(('ep', 'tp'), None)
    in_specs = (tok_spec, tok_spec, P(None, None), P('ep', None, 'tp'), P('ep', None, 'tp'), P('ep', 'tp', None), P(None, 'tp'), P(None, 'tp'), P('tp', None), tok_spec)
    out_specs = (tok_spec, tok_spec, P(None, None), P('ep', None, 'tp'), P('ep', None, 'tp'), P('ep', 'tp', None), P(None, 'tp'), P(None, 'tp'), P('tp', None))
    return jax.shard_map(device_step, mesh=mesh, in_specs=in_specs, out_specs=out_specs, check_vma=False)
```

profile of v0, /device:TPU:0, one launch (start us, length us, event | category | flops | bytes accessed | tf_op | source)
XLA Modules:
  0.0 1238.5 jit_solution(9278420441017187168)
XLA Ops:
  10.3 7.5 gather_fusion.1
  18.5 8.1 scatter_custom_fusion
  26.6 6.0 gather_fusion.2
  36.6 7.1 reshape.82
  47.4 52.1 %all_to_all.20 = bf16[4,16,21,1536]{3,1,2,0:T(8,128)(2,1)} all-to-all(bf16[4,16,21,1536]{3,1,2,0:T(8,128)(2,1)S(1)} %copy.120), channel_id=1, replica_groups=mesh['tp'=2,'ep'=4] {'ep'}, dimensions={0} | all-to-all | bytes 8257536 | tf_op jit(solution)/shard_map/all_to_all | solution.py:48
  99.8 101.2 %all-gather.11.cloned.1.call-done = bf16[8,16,21,1536]{3,1,2,0:T(8,128)(2,1)} async-done(((bf16[4,16,21,1536]{3,1,2,0:T(8,128)(2,1)}), bf16[8,16,21,1536]{3,1,2,0:T(8,128)(2,1)}) %all-gather.11.cloned.1.call-update) | async-done | bytes 8257552 | tf_op jit(solution)/shard_map/all_gather | solution.py:49
  201.1 11.7 copy.121
  212.8 10.5 fusion.37
  223.3 12.7 %fusion.26 = (bf16[2,4,16,21,256]{4,3,1,0,2:T(8,128)(2,1)S(1)}, bf16[16,2,4,21,256]{4,3,2,1,0:T(8,128)(2,1)}) fusion(bf16[16,2,4,21,256]{4,3,2,1,0:T(8,128)(2,1)S(1)} %fusion.37, bf16[2,4,16,21,1536]{4,3,1,0,2:T(8,128)(2,1)} %bitcast.153, bf16[16,1536,256]{2,1,0:T(8,128)(2,1)} %param.18), kind=kOutput, calls=%fused_computation.46 | convolution fusion | flops 2120122368 | bytes 24969216 | tf_op jit(solution)/shard_map/tsecd,edf->tsecf/dot_general | solution.py:51
  236.0 15.2 %fusion.17 = f32[2,4,16,21,1536]{4,3,1,0,2:T(8,128)} fusion(bf16[2,4,16,21,256]{4,3,1,0,2:T(8,128)(2,1)S(1)} %get-tuple-element.68, bf16[16,256,1536]{2,1,0:T(8,128)(2,1)} %param.19), kind=kOutput, calls=%fused_computation.28 | convolution fusion | flops 2113929216 | bytes 30474240 | tf_op jit(solution)/shard_map/tsecf,efd->tsecd/dot_general | solution.py:53
  251.2 17.9 %copy.122 = f32[2,4,16,21,1536]{4,2,3,1,0:T(8,128)} copy(f32[2,4,16,21,1536]{4,3,1,0,2:T(8,128)} %fusion.17) | data formatting | bytes 33030144 | tf_op jit(solution)/shard_map/tsecf,efd->tsecd/transpose | solution.py:53
  269.2 183.6 %reduce-scatter.7.cloned.1.call-done = f32[1,4,16,21,1536]{4,2,3,1,0:T(8,128)} async-done(((f32[2,4,16,21,1536]{4,2,3,1,0:T(8,128)}), f32[1,4,16,21,1536]{4,2,3,1,0:T(8,128)}) %reduce-scatter.7.cloned.1.call-update) | async-done | bytes 8257552 | tf_op jit(solution)/shard_map/reduce_scatter | solution.py:54
  452.8 6.0 convert_bitcast_fusion.1
  458.8 4.9 all-to-all-start.1
  464.2 6.0 gather_fusion.4
  470.6 40.3 %all-to-all-done.1 = bf16[4,16,21,1536]{3,1,2,0:T(8,128)(2,1)} async-done(((bf16[4,16,21,1536]{3,1,2,0:T(8,128)(2,1)}), bf16[4,16,21,1536]{3,1,2,0:T(8,128)(2,1)}, u32[]{:S(2)}, u32[]{:S(2)}) %all-to-all-start.1) | async-done | bytes 4128800 | tf_op jit(solution)/shard_map/all_to_all | solution.py:55
  510.9 6.7 copy.123
  517.6 7.2 reshape.83
  524.8 11.5 gather_fusion.3
  536.2 6.6 reshape.166
  542.9 5.9 fusion.20
  549.0 9.3 gather_fusion
  558.8 8.3 scatter_custom_fusion.1
  567.1 4.2 multiply_convert_fusion
  571.3 7.1 reshape.84
  578.4 5.7 copy.127
  584.1 4.9 all-to-all-start.2
  590.4 45.8 %all-to-all-done.2 = bf16[4,16,21,1536]{3,1,2,0:T(8,128)(2,1)} async-done(((bf16[4,16,21,1536]{3,1,2,0:T(8,128)(2,1)}), bf16[4,16,21,1536]{3,1,2,0:T(8,128)(2,1)}, u32[]{:S(2)}, u32[]{:S(2)}) %all-to-all-start.2) | async-done | bytes 4128800 | tf_op jit(solution)/shard_map/all_to_all | solution.py:67
  656.0 80.1 %all-gather.13.cloned.1.call-done = bf16[8,16,21,1536]{3,1,2,0:T(8,128)(2,1)} async-done(((bf16[4,16,21,1536]{3,1,2,0:T(8,128)(2,1)}), bf16[8,16,21,1536]{3,1,2,0:T(8,128)(2,1)}) %all-gather.13.cloned.1.call-update) | async-done | bytes 8257552 | tf_op jit(solution)/shard_map/all_gather | solution.py:68
  736.1 11.7 copy.128
  747.8 15.1 %fusion.24 = (bf16[2,4,16,21,256]{4,3,1,0,2:T(8,128)(2,1)S(1)}, bf16[2,4,16,21,256]{4,3,1,0,2:T(8,128)(2,1)S(1)}) fusion(bf16[16,2,4,21,256]{4,3,2,1,0:T(8,128)(2,1)} %copy-done.21, bf16[16,2,4,21,256]{4,3,2,1,0:T(8,128)(2,1)} %get-tuple-element.69, bf16[2,4,16,21,1536]{4,3,1,0,2:T(8,128)(2,1)} %bitcast.151, bf16[16,256,1536]{2,1,0:T(8,128)(2,1)} %param.19), kind=kOutput, calls=%fused_computation.41 | convolution fusion | flops 2126315520 | bytes 26345472 | tf_op jit(solution)/shard_map/tsecd,efd->tsecf/dot_general | solution.py:69
  762.9 16.2 %fusion = f32[16,2,4,21,1536]{4,3,2,1,0:T(8,128)} fusion(bf16[2,4,16,21,256]{4,3,1,0,2:T(8,128)(2,1)S(1)} %get-tuple-element.64, bf16[16,1536,256]{2,1,0:T(8,128)(2,1)} %param.18), kind=kOutput, calls=%fused_computation.12 | convolution fusion | flops 2113929216 | bytes 30474240 | tf_op jit(solution)/shard_map/tsecf,edf->tsecd/dot_general | solution.py:77
  779.1 19.9 %add_bitcast_fusion = f32[2,4,16,21,1536]{4,3,1,0,2:T(8,128)} fusion(f32[16,2,4,21,1536]{4,3,2,1,0:T(8,128)} %fusion, bf16[2,4,16,21,256]{4,3,1,0,2:T(8,128)(2,1)S(1)} %get-tuple-element.63, bf16[16,1536,256]{2,1,0:T(8,128)(2,1)} %param.17), kind=kOutput, calls=%fused_computation.8 | convolution fusion | flops 2118057984 | bytes 46989312 | tf_op jit(solution)/shard_map/tsecf,edf->tsecd/dot_general | solution.py:77
  799.0 17.9 %copy.129 = f32[2,4,16,21,1536]{4,2,3,1,0:T(8,128)} copy(f32[2,4,16,21,1536]{4,3,1,0,2:T(8,128)} %add_bitcast_fusion) | data formatting | bytes 33030144 | tf_op jit(solution)/shard_map/add | solution.py:77
  822.6 81.3 %all-reduce.7.cloned.1.call-done = (f32[1536,512]{0,1:T(8,128)}, f32[1536,512]{0,1:T(8,128)}, f32[512,1536]{1,0:T(8,128)}) async-done(((f32[1536,512]{0,1:T(8,128)}, f32[1536,512]{0,1:T(8,128)}, f32[512,1536]{1,0:T(8,128)}), (f32[1536,512]{0,1:T(8,128)}, f32[1536,512]{0,1:T(8,128)}, f32[512,1536]{1,0:T(8,128)})) %all-reduce.7.cloned.1.call-update) | async-done | bytes 9437200 | tf_op jit(solution)/shard_map/psum | solution.py:92
  912.2 4.8 fusion.21
  917.1 21.2 %reduce-scatter.5.cloned.1.call-done = f32[192,1536]{1,0:T(8,128)} async-done(((f32[384,1536]{1,0:T(8,128)}), f32[192,1536]{1,0:T(8,128)}) %reduce-scatter.5.cloned.1.call-update) | async-done | bytes 1179664 | tf_op jit(solution)/shard_map/reduce_scatter | solution.py:62
  940.8 17.0 %convolution_bitcast_fusion.1 = f32[16,1536,256]{2,1,0:T(8,128)} fusion(bf16[2,4,16,21,1536]{4,2,3,1,0:T(8,128)(2,1)} %bitcast.154, bf16[2,4,16,21,256]{4,3,1,0,2:T(8,128)(2,1)S(1)} %copy-done.13), kind=kOutput, calls=%fused_computation.10 | convolution fusion | flops 2113929216 | bytes 34799616 | tf_op jit(solution)/shard_map/tsecd,tsecf->edf/dot_general | solution.py:76
  957.8 166.8 %reduce-scatter.11.cloned.1.call-done = f32[1,4,16,21,1536]{4,2,3,1,0:T(8,128)} async-done(((f32[2,4,16,21,1536]{4,2,3,1,0:T(8,128)}), f32[1,4,16,21,1536]{4,2,3,1,0:T(8,128)}) %reduce-scatter.11.cloned.1.call-update) | async-done | bytes 8257552 | tf_op jit(solution)/shard_map/reduce_scatter | solution.py:78
  1124.6 5.9 convert_bitcast_fusion
  1130.5 4.9 all-to-all-start.3
  1135.5 17.2 %convolution_bitcast_fusion.2 = f32[16,1536,256]{2,1,0:T(8,128)} fusion(bf16[2,4,16,21,1536]{4,2,3,1,0:T(8,128)(2,1)} %bitcast.155, bf16[2,4,16,21,256]{4,3,1,0,2:T(8,128)(2,1)S(1)} %get-tuple-element.63), kind=kOutput, calls=%fused_computation.11 | convolution fusion | flops 2113929216 | bytes 34799616 | tf_op jit(solution)/shard_map/tsecd,tsecf->edf/dot_general | solution.py:75
  1152.6 28.7 %convolution_bitcast_fusion = f32[16,256,1536]{2,1,0:T(8,128)} fusion(bf16[2,4,16,21,1536]{4,2,3,1,0:T(8,128)(2,1)} %bitcast.156, bf16[2,4,16,21,256]{4,3,1,0,2:T(8,128)(2,1)S(1)} %copy-done.15), kind=kOutput, calls=%fused_computation.9 | convolution fusion | flops 2113929216 | bytes 34799616 | tf_op jit(solution)/shard_map/tsecf,tsecd->efd/dot_general | solution.py:70
  1184.7 6.6 copy.130
  1191.3 7.2 reshape.85
  1198.6 11.4 gather_fusion.5
  1210.0 6.6 reshape.172
  1216.7 6.4 convert_reduce_fusion
  (126 shorter events, 62.2 us)
Async XLA Ops:
  7.2 635.7 %copy-start = (bf16[512,1536]{1,0:T(8,128)(2,1)S(1)}, bf16[512,1536]{1,0:T(8,128)(2,1)}, u32[]{:S(2)}) copy-start(bf16[512,1536]{1,0:T(8,128)(2,1)} %param.22) | copy-start | bytes 4718596
  7.2 193.9 %all-gather.11.cloned.1.call-start = ((), (), s32[]{:S(2)}) async-start(), calls=%async_computation.15 | async-start | bytes 12386304 | tf_op jit(solution)/shard_map/all_gather | solution.py:49
  10.3 7.8 copy-start.20
  17.8 8.8 copy-start.2
  99.6 353.2 %reduce-scatter.7.cloned.1.call-start = ((), (), s32[]{:S(2)}) async-start(), calls=%async_computation.10 | async-start | bytes 24772608 | tf_op jit(solution)/shard_map/reduce_scatter | solution.py:54
  223.3 12.7 %copy-start.21 = (bf16[16,2,4,21,256]{4,3,2,1,0:T(8,128)(2,1)}, bf16[16,2,4,21,256]{4,3,2,1,0:T(8,128)(2,1)S(1)}, u32[]{:S(2)}) copy-start(bf16[16,2,4,21,256]{4,3,2,1,0:T(8,128)(2,1)S(1)} %fusion.37) | copy-start | bytes 4128772
  236.0 15.2 %copy-start.14 = (bf16[2,4,16,21,256]{4,3,1,0,2:T(8,128)(2,1)}, bf16[2,4,16,21,256]{4,3,1,0,2:T(8,128)(2,1)S(1)}, u32[]{:S(2)}) copy-start(bf16[2,4,16,21,256]{4,3,1,0,2:T(8,128)(2,1)S(1)} %get-tuple-element.68) | copy-start | bytes 4128772
  458.8 5.4 copy-start.4
  458.8 52.1 %all-to-all-start.1 = ((bf16[4,16,21,1536]{3,1,2,0:T(8,128)(2,1)}), bf16[4,16,21,1536]{3,1,2,0:T(8,128)(2,1)}, u32[]{:S(2)}, u32[]{:S(2)}) async-start(bf16[4,16,21,1536]{3,1,2,0:T(8,128)(2,1)} %convert_bitcast_fusion.1), calls=%async_computation.3 | async-start | bytes 8257536 | tf_op jit(solution)/shard_map/all_to_all | solution.py:55
  464.2 6.0 copy-start.18
  470.2 54.6 %copy-start.5 = (s32[2048]{0:T(1024)}, s32[2048]{0:T(1024)S(1)}, u32[]{:S(2)}) copy-start(s32[2048]{0:T(1024)S(1)} %pad_clamp_fusion) | copy-start | bytes 24580
  584.1 52.0 %all-to-all-start.2 = ((bf16[4,16,21,1536]{3,1,2,0:T(8,128)(2,1)}), bf16[4,16,21,1536]{3,1,2,0:T(8,128)(2,1)}, u32[]{:S(2)}, u32[]{:S(2)}) async-start(bf16[4,16,21,1536]{3,1,2,0:T(8,128)(2,1)} %copy.127), calls=%async_computation.5 | async-start | bytes 8257536 | tf_op jit(solution)/shard_map/all_to_all | solution.py:67
  589.0 47.3 %all-gather.7.cloned.1.call-start = ((), (), s32[]{:S(2)}) async-start(), calls=%async_computation.8 | async-start | bytes 1769472 | tf_op jit(solution)/shard_map/all_gather | solution.py:58
  589.7 53.1 %all-gather.9.cloned.1.call-start = ((), (), s32[]{:S(2)}) async-start(), calls=%async_computation.11 | async-start | bytes 1769472 | tf_op jit(solution)/shard_map/all_gather | solution.py:85
  590.3 145.7 %all-gather.13.cloned.1.call-start = ((), (), s32[]{:S(2)}) async-start(), calls=%async_computation.16 | async-start | bytes 12386304 | tf_op jit(solution)/shard_map/all_gather | solution.py:68
  636.2 267.7 %all-reduce.7.cloned.1.call-start = ((), (), s32[]{:S(2)}) async-start(), calls=%async_computation.17 | async-start | bytes 18874368 | tf_op jit(solution)/shard_map/psum | solution.py:92
  636.3 3.5 copy-start.7
  645.6 2.7 copy-start.8
  645.7 2.7 copy-start.10
  648.3 2.7 copy-start.17
  653.7 284.5 %reduce-scatter.5.cloned.1.call-start = ((), (), s32[]{:S(2)}) async-start(), calls=%async_computation.9 | async-start | bytes 3538944 | tf_op jit(solution)/shard_map/reduce_scatter | solution.py:62
  655.9 468.7 %reduce-scatter.11.cloned.1.call-start = ((), (), s32[]{:S(2)}) async-start(), calls=%async_computation.13 | async-start | bytes 24772608 | tf_op jit(solution)/shard_map/reduce_scatter | solution.py:78
  762.9 16.2 %copy-start.12 = (bf16[2,4,16,21,256]{4,3,1,0,2:T(8,128)(2,1)}, bf16[2,4,16,21,256]{4,3,1,0,2:T(8,128)(2,1)S(1)}, u32[]{:S(2)}) copy-start(bf16[2,4,16,21,256]{4,3,1,0,2:T(8,128)(2,1)S(1)} %get-tuple-element.64) | copy-start | bytes 4128772
  817.0 1.0 copy-start.11
  817.0 3.3 copy-start.9
  817.0 406.2 %reduce-scatter.9.cloned.1.call-start = ((), (), s32[]{:S(2)}) async-start(), calls=%async_computation.12 | async-start | bytes 3538944 | tf_op jit(solution)/shard_map/reduce_scatter | solution.py:95
  818.0 2.3 copy-start.16
  822.6 403.0 %all-reduce.5.cloned.1.call-start = ((), (), s32[]{:S(2)}) async-start(), calls=%async_computation.14 | async-start | bytes 786432 | tf_op jit(solution)/shard_map/psum | solution.py:83
  907.4 3.8 copy-start.3
  917.0 23.8 %copy-start.13 = (bf16[2,4,16,21,256]{4,3,1,0,2:T(8,128)(2,1)S(1)}, bf16[2,4,16,21,256]{4,3,1,0,2:T(8,128)(2,1)}, u32[]{:S(2)}) copy-start(bf16[2,4,16,21,256]{4,3,1,0,2:T(8,128)(2,1)} %copy-done.12) | copy-start | bytes 4128772
  1130.5 54.2 %all-to-all-start.3 = ((bf16[4,16,21,1536]{3,1,2,0:T(8,128)(2,1)}), bf16[4,16,21,1536]{3,1,2,0:T(8,128)(2,1)}, u32[]{:S(2)}, u32[]{:S(2)}) async-start(bf16[4,16,21,1536]{3,1,2,0:T(8,128)(2,1)} %convert_bitcast_fusion), calls=%async_computation.7 | async-start | bytes 8257536 | tf_op jit(solution)/shard_map/all_to_all | solution.py:79
  1135.4 17.2 %copy-start.15 = (bf16[2,4,16,21,256]{4,3,1,0,2:T(8,128)(2,1)S(1)}, bf16[2,4,16,21,256]{4,3,1,0,2:T(8,128)(2,1)}, u32[]{:S(2)}) copy-start(bf16[2,4,16,21,256]{4,3,1,0,2:T(8,128)(2,1)} %copy-done.14) | copy-start | bytes 4128772
  1191.3 7.3 copy-start.6
  1216.7 6.5 copy-start.19
  1225.6 5.6 copy-start.1
Sparse Core Ops, SparseCore 0:
  99.7 101.3 all-gather.10
  269.3 183.4 reduce-scatter.6
  591.3 20.1 all-gather.6
  612.8 19.6 all-gather.8
  636.3 99.6 all-gather.12
  739.8 164.0 all-reduce.6
  906.1 32.0 reduce-scatter.4
  941.1 183.5 reduce-scatter.10
  1126.8 31.8 reduce-scatter.8
  1162.2 43.6 all-reduce.4
where the time goes:
time: 1250 us; the launch traced here: 1240 us
  waiting for transfers between devices  725 us (58%)
  local copies, waits for them, and re-layouts  192 us (15%)
  matrix products  191 us (15%)
  blocking collectives  52.1 us (4%)
  other arithmetic  48 us (4%)
  starting transfers between devices  15.5 us (1%)
  between operations  15.1 us (1%)
    reduce_scatter x1, waiting for transfers between devices, device_step(): lax.psum_scatter(part_out, 'tp', scatter_dimension=0).astype(jnp.bfloat16)  184 us
    reduce_scatter x1, waiting for transfers between devices, device_step(): lax.psum_scatter(d_rows_part, 'tp', scatter_dimension=0)  167 us
    all_gather x1, waiting for transfers between devices, device_step(): expert_rows = lax.all_gather(recv_rows, 'tp', axis=0)  101 us
    psum x1, waiting for transfers between devices, device_step(): lax.psum(jnp.einsum('td,tf->df', x_group, dsg_pre, preferred_element_type...  81.3 us
    all_gather x1, waiting for transfers between devices, device_step(): d_rows_in = lax.all_gather(d_recv, 'tp', axis=0)  80.1 us
    all_to_all x1, blocking collectives, device_step(): recv_rows = lax.all_to_all(send_rows, 'ep', 0, 0)  52.1 us
    all_to_all x1, waiting for transfers between devices, device_step(): lax.all_to_all(d_out.reshape(ep_size, local_exp, capacity_rows, model_dim...  45.8 us
    all_to_all x1, waiting for transfers between devices, device_step(): back_rows = lax.all_to_all(own_out, 'ep', 0, 0).reshape(n_slots, model_dim)  40.3 us
  transfers between devices with their start and end apart: 13, of which 9 were waited for; matrix products, arithmetic and copies ran while one was open for 19% of the time, Pallas kernels for 0%

commit v1 on v0

v1 whole, which is shorter than its diff:
```python
import functools

import jax
import jax.numpy as jnp
from jax import lax
from jax.experimental import pallas as pl
from jax.experimental.pallas import tpu as pltpu
from jax.sharding import PartitionSpec as P

GATE_SCALE = 16.0
BF16 = jnp.bfloat16
F32 = jnp.float32
FWD_CHUNKS = (2, 4, 10)
BWD_CHUNKS = (10, 4, 2)

NN = (((1,), (0,)), ((), ()))
NT = (((1,), (1,)), ((), ()))
TN = (((0,), (0,)), ((), ()))


def dot(a, b, dims=NN):
    return lax.dot_general(a, b, dims, preferred_element_type=F32)


def sigmoid(v):
    return 1.0 / (1.0 + jnp.exp(-jnp.maximum(v, -88.0)))


def swiglu_fwd(a, b):
    return (a * sigmoid(a) * b).astype(BF16)


def swiglu_bwd(a, b, dh):
    sig = sigmoid(a)
    silu = a * sig
    h = (silu * b).astype(BF16)
    da = (dh * b * (sig * (1.0 + a * (1.0 - sig)))).astype(BF16)
    db = (dh * silu).astype(BF16)
    return h, da, db


def rounded(v):
    return v.astype(BF16).astype(F32)


def half_rows(cap, ep_size):
    half = cap * ep_size
    return half, half + (-half) % 8


def store_parts(parity, part, send_ref, own_ref, half, padded):
    shift = padded - half

    @pl.when(parity == 0)
    def _():
        send_ref[0:half, :] = part[0:half]
        own_ref[0:half, :] = part[padded:padded + half]

    @pl.when(parity == 1)
    def _():
        send_ref[half:2 * half, :] = part[shift:padded]
        own_ref[half:2 * half, :] = part[padded + shift:2 * padded]


def pick_matrix(row_ref, rows):
    ids = row_ref[0]
    iota = lax.broadcasted_iota(jnp.int32, (rows, ids.shape[1]), 0)
    return iota == ids


def fwd_kernel(half, padded, x_ref, row_ref, w1_ref, w3_ref, w2_ref, send_ref, own_ref):
    hit = pick_matrix(row_ref, 2 * padded)
    rows = dot(jnp.where(hit, 1.0, 0.0).astype(BF16), x_ref[...]).astype(BF16)
    a = rounded(dot(rows, w1_ref[0]))
    b = rounded(dot(rows, w3_ref[0]))
    h = swiglu_fwd(a, b)
    part = dot(h, w2_ref[0])
    store_parts(pl.program_id(0) % 2, part, send_ref, own_ref, half, padded)


def bwd_kernel(half, padded, starts, x_ref, dy_ref, row_ref, gate_ref, w1_ref, w3_ref, w2_ref, *outs):
    dw1_ref, dw3_ref, dw2_ref = outs[:3]
    e = pl.program_id(0)
    hit = pick_matrix(row_ref, 2 * padded)
    pick = jnp.where(hit, 1.0, 0.0).astype(BF16)
    rows = dot(pick, x_ref[...]).astype(BF16)
    gates = jnp.sum(jnp.where(hit, gate_ref[0], 0.0), axis=1, keepdims=True)
    d_out = (dot(pick, dy_ref[...]) * gates).astype(BF16)
    a = rounded(dot(rows, w1_ref[0]))
    b = rounded(dot(rows, w3_ref[0]))
    dh = rounded(dot(d_out, w2_ref[0], NT))
    h, da, db = swiglu_bwd(a, b, dh)
    dw2_ref[0] = dot(h, d_out, TN)
    dw1_ref[0] = dot(rows, da, TN)
    dw3_ref[0] = dot(rows, db, TN)
    part = dot(da, w1_ref[0], NT) + dot(db, w3_ref[0], NT)
    for j in range(len(starts) - 1):
        @pl.when((e >= starts[j]) & (e < starts[j + 1]))
        def _():
            store_parts(e % 2, part, outs[3 + 2 * j], outs[4 + 2 * j], half, padded)


def expert_fwd(start, count, half, padded, x_all, row_ids, w_gate, w_up, w_down):
    tokens, model = x_all.shape
    width = w_gate.shape[2]
    out = jax.ShapeDtypeStruct((count * half, model), F32)
    return pl.pallas_call(
        functools.partial(fwd_kernel, half, padded),
        grid=(count,),
        in_specs=[
            pl.BlockSpec((tokens, model), lambda i: (0, 0), pipeline_mode=pl.Buffered(1)),
            pl.BlockSpec((1, 1, tokens), lambda i: (start + i, 0, 0)),
            pl.BlockSpec((1, model, width), lambda i: (start + i, 0, 0)),
            pl.BlockSpec((1, model, width), lambda i: (start + i, 0, 0)),
            pl.BlockSpec((1, width, model), lambda i: (start + i, 0, 0)),
        ],
        out_specs=[pl.BlockSpec((2 * half, model), lambda i: (i // 2, 0))] * 2,
        out_shape=[out, out],
        cost_estimate=pl.CostEstimate(
            flops=count * 2 * 2 * padded * model * (tokens + 3 * width),
            bytes_accessed=count * (6 * model * width + 8 * half * model) + 2 * tokens * model,
            transcendentals=count * 2 * padded * width),
        compiler_params=pltpu.CompilerParams(dimension_semantics=('arbitrary',), vmem_limit_bytes=48 << 20),
        name='expert_fwd_%d' % start,
    )(x_all, row_ids, w_gate, w_up, w_down)


def expert_bwd(chunks, half, padded, x_all, dy_all, row_ids, gates, w_gate, w_up, w_down):
    tokens, model = x_all.shape
    count, _, width = w_gate.shape
    starts = [0]
    for c in chunks:
        starts.append(starts[-1] + c)

    def chunk_spec(j):
        lo, n = starts[j] // 2, chunks[j] // 2
        return pl.BlockSpec((2 * half, model), lambda i: (jnp.clip(i // 2 - lo, 0, n - 1), 0))

    part_specs, part_shapes = [], []
    for j, c in enumerate(chunks):
        part_specs += [chunk_spec(j)] * 2
        part_shapes += [jax.ShapeDtypeStruct((c * half, model), F32)] * 2
    outs = pl.pallas_call(
        functools.partial(bwd_kernel, half, padded, starts),
        grid=(count,),
        in_specs=[
            pl.BlockSpec((tokens, model), lambda i: (0, 0), pipeline_mode=pl.Buffered(1)),
            pl.BlockSpec((tokens, model), lambda i: (0, 0), pipeline_mode=pl.Buffered(1)),
            pl.BlockSpec((1, 1, tokens), lambda i: (i, 0, 0)),
            pl.BlockSpec((1, 1, tokens), lambda i: (i, 0, 0)),
            pl.BlockSpec((1, model, width), lambda i: (i, 0, 0)),
            pl.BlockSpec((1, model, width), lambda i: (i, 0, 0)),
            pl.BlockSpec((1, width, model), lambda i: (i, 0, 0)),
        ],
        out_specs=[
            pl.BlockSpec((1, model, width), lambda i: (i, 0, 0)),
            pl.BlockSpec((1, model, width), lambda i: (i, 0, 0)),
            pl.BlockSpec((1, width, model), lambda i: (i, 0, 0)),
        ] + part_specs,
        out_shape=[
            jax.ShapeDtypeStruct((count, model, width), F32),
            jax.ShapeDtypeStruct((count, model, width), F32),
            jax.ShapeDtypeStruct((count, width, model), F32),
        ] + part_shapes,
        cost_estimate=pl.CostEstimate(
            flops=count * 2 * 2 * padded * model * (2 * tokens + 8 * width),
            bytes_accessed=count * (18 * model * width + 8 * half * model) + 4 * tokens * model,
            transcendentals=count * 2 * padded * width),
        compiler_params=pltpu.CompilerParams(dimension_semantics=('arbitrary',), vmem_limit_bytes=60 << 20),
        name='expert_bwd',
    )(x_all, dy_all, row_ids, gates, w_gate, w_up, w_down)
    return outs[:3], [(outs[3 + 2 * j], outs[4 + 2 * j]) for j in range(len(chunks))]


def split3(v):
    hi = lax.reduce_precision(v, 8, 7)
    rest = v - hi
    mid = lax.reduce_precision(rest, 8, 7)
    low = rest - mid
    return hi.astype(BF16), mid.astype(BF16), low.astype(BF16)


def solution(mesh):
    tp_size = mesh.shape['tp']
    ep_size = mesh.shape['ep']
    swap = [(i, tp_size - 1 - i) for i in range(tp_size)]

    def device_step(x, grad_y, w_router, w_gate, w_up, w_down, ws_gate, ws_up, ws_down, topk_idx):
        tok, model = x.shape
        top_k = topk_idx.shape[1]
        experts = w_router.shape[1]
        local_exp = w_gate.shape[0]
        groups = top_k // 2
        most = groups * tok // (2 * ep_size) + min(groups, ep_size // 2) * tok // ep_size
        cap = (2 * most + local_exp - 1) // local_exp
        half, padded = half_rows(cap, ep_size)
        shift = padded - half
        ep_i = lax.axis_index('ep')
        tp_i = lax.axis_index('tp')
        devices = ep_size * tp_size

        x_all = lax.all_gather(x, ('ep', 'tp'), axis=0, tiled=True)
        idx_all = lax.all_gather(topk_idx, ('ep', 'tp'), axis=0, tiled=True)
        dy_all = lax.all_gather(grad_y, ('ep', 'tp'), axis=0, tiled=True)

        lower = (lax.broadcasted_iota(jnp.int32, (tok, tok), 0) > lax.broadcasted_iota(jnp.int32, (tok, tok), 1)).astype(BF16)
        local_ids = ep_i * local_exp + jnp.arange(local_exp, dtype=jnp.int32)
        hit = jnp.any(idx_all.reshape(devices, 1, tok, top_k) == local_ids[None, :, None, None], axis=3)
        rank = jnp.einsum('dej,ij->edi', hit.astype(BF16), lower, preferred_element_type=F32).astype(jnp.int32)
        dev = jnp.arange(devices, dtype=jnp.int32)
        is_own = (dev % tp_size) == tp_i
        parity = jnp.arange(local_exp, dtype=jnp.int32) % 2
        base = (jnp.where(is_own, padded, 0) + (dev // tp_size) * cap)[None, :] + (parity * shift)[:, None]
        row_ids = jnp.where(jnp.transpose(hit, (1, 0, 2)), base[:, :, None] + rank, -1).reshape(local_exp, 1, devices * tok)

        fwd_parts = []
        start = 0
        for count in FWD_CHUNKS:
            send, own = expert_fwd(start, count, half, padded, x_all, row_ids, w_gate, w_up, w_down)
            fwd_parts.append((lax.ppermute(send, 'tp', swap), own))
            start += count

        logits_t = jnp.einsum('de,td->et', w_router, x_all, preferred_element_type=F32)
        probs_t = jax.nn.softmax(logits_t, axis=0)
        gates_local = GATE_SCALE * lax.dynamic_slice_in_dim(probs_t, ep_i * local_exp, local_exp, 0).reshape(local_exp, 1, devices * tok)

        (d_w_gate, d_w_up, d_w_down), bwd_out = expert_bwd(BWD_CHUNKS, half, padded, x_all, dy_all, row_ids, gates_local, w_gate, w_up, w_down)
        bwd_parts = [(lax.ppermute(send, 'tp', swap), own) for send, own in bwd_out]

        def other_half(w):
            n = w.shape[0] // ep_size
            quarter = lax.dynamic_slice_in_dim(w, ep_i * n, n, 0)
            return lax.all_gather(lax.ppermute(quarter, 'tp', swap), 'ep', axis=0, tiled=True)

        ws_other = (other_half(ws_gate), other_half(ws_up), other_half(ws_down))

        shared = jnp.zeros((tok, model), F32)
        dx_shared = jnp.zeros((tok, model), F32)
        for wg, wu, wd in ((ws_gate, ws_up, ws_down), ws_other):
            a = rounded(dot(x, wg))
            b = rounded(dot(x, wu))
            dh = rounded(dot(grad_y, wd, NT))
            h, da, db = swiglu_bwd(a, b, dh)
            shared = shared + dot(h, wd)
            dx_shared = dx_shared + dot(da, wg, NT) + dot(db, wu, NT)
        a = rounded(dot(x_all, ws_gate))
        b = rounded(dot(x_all, ws_up))
        dh = rounded(dot(dy_all, ws_down, NT))
        h, da, db = swiglu_bwd(a, b, dh)
        ds_down = dot(h, dy_all, TN)
        ds_gate = dot(x_all, da, TN)
        ds_up = dot(x_all, db, TN)

        def give_back(parts, count):
            recv, own = parts
            rows = (recv + own).astype(BF16)
            new = jnp.arange(ep_size * count * cap, dtype=jnp.int32)
            src, rest = new // (count * cap), new % (count * cap)
            old = (rest // cap) * half + src * cap + rest % cap
            perm = (old[:, None] == jnp.arange(count * half, dtype=jnp.int32)[None, :]).astype(BF16)
            out = dot(perm, rows).astype(BF16).reshape(ep_size, count * cap, model)
            return lax.all_to_all(out, 'ep', 0, 0).reshape(ep_size * count * cap, model)

        hit_own = jnp.any(topk_idx[:, None, :] == jnp.arange(experts, dtype=jnp.int32)[None, :, None], axis=2)
        rank_own = dot(lower, hit_own.astype(BF16)).astype(jnp.int32)
        probs = jax.nn.softmax(dot(x, w_router), axis=-1)

        def columns(v, start, count):
            picked = v.reshape(tok, ep_size, local_exp)[:, :, start:start + count]
            return jnp.broadcast_to(picked[..., None], (tok, ep_size, count, cap)).reshape(tok, ep_size * count * cap)

        def slot_hits(start, count):
            slot = jnp.arange(ep_size * count * cap, dtype=jnp.int32) % cap
            want = jnp.where(hit_own, rank_own, -1)
            return columns(want, start, count) == slot[None, :]

        routed = jnp.zeros((tok, model), F32)
        d_scores = []
        start = 0
        for parts, count in zip(fwd_parts, FWD_CHUNKS):
            back = give_back(parts, count)
            hits = slot_hits(start, count)
            gates = jnp.where(hits, GATE_SCALE * columns(probs, start, count), 0.0)
            for piece in split3(gates):
                routed = routed + dot(piece, back)
            score = jnp.where(hits, dot(grad_y, back, NT), 0.0)
            d_scores.append(jnp.sum(score.reshape(tok, ep_size, count, cap), axis=3))
            start += count
        y_out = (shared + routed).astype(BF16)

        d_scores = GATE_SCALE * jnp.concatenate(d_scores, axis=2).reshape(tok, experts)
        d_logits = probs * (d_scores - jnp.sum(probs * d_scores, axis=-1, keepdims=True))
        d_router = lax.psum(jnp.einsum('td,te->de', x, d_logits, preferred_element_type=F32), ('tp', 'ep'))
        dx_sum = jnp.einsum('te,de->td', d_logits, w_router, preferred_element_type=F32) + dx_shared

        start = 0
        for parts, count in zip(bwd_parts, BWD_CHUNKS):
            back = give_back(parts, count)
            dx_sum = dx_sum + dot(slot_hits(start, count).astype(BF16), back)
            start += count
        return y_out, dx_sum.astype(BF16), d_router, d_w_gate, d_w_up, d_w_down, ds_gate, ds_up, ds_down

    tok_spec = P(('ep', 'tp'), None)
    in_specs = (tok_spec, tok_spec, P(None, None), P('ep', None, 'tp'), P('ep', None, 'tp'), P('ep', 'tp', None), P(None, 'tp'), P(None, 'tp'), P('tp', None), tok_spec)
    out_specs = (tok_spec, tok_spec, P(None, None), P('ep', None, 'tp'), P('ep', None, 'tp'), P('ep', 'tp', None), P(None, 'tp'), P(None, 'tp'), P('tp', None))
    return jax.shard_map(device_step, mesh=mesh, in_specs=in_specs, out_specs=out_specs, check_vma=False)
```

time: 1250 us -> 608 us (0.49)
  waiting for transfers between devices: 725 us -> 232 us
  local copies, waits for them, and re-layouts: 192 us -> 75.4 us
  Pallas kernels: 0 us -> 112 us
  matrix products: 191 us -> 107 us
  blocking collectives: 52.1 us -> 12.1 us
  other arithmetic: 48 us -> 11.1 us
  starting transfers between devices: 15.5 us -> 36.3 us
    reduce_scatter x4 -> x0, waiting for transfers between devices: 372 us -> none  [the longest x1 184 us: device_step(): lax.psum_scatter(part_out, 'tp', scatter_dimension=0).astype(jnp.bfloat16)]
    ppermute x0 -> x9, waiting for transfers between devices: none -> 178 us  [the longest x3 76.9 us: device_step(): fwd_parts.append((lax.ppermute(send, 'tp', swap), own))]
    all_gather x4 -> x5, waiting for transfers between devices: 181 us -> 26.9 us  [the longest x1 26.9 us: device_step(): x_all = lax.all_gather(x, ('ep', 'tp'), axis=0, tiled=True)]
    pallas_call x0 -> x4, Pallas kernels: none -> 112 us  [the longest x1 70 us: expert_bwd(): pl.pallas_call(functools.partial(bwd_kernel, half, padded, starts), grid=...]
    dot_general x23 -> x45, matrix products: 191 us -> 107 us  [the longest x41 103 us: dot(): return lax.dot_general(a, b, dims, preferred_element_type=F32)]
    all_to_all x3 -> x6, waiting for transfers between devices: 89.6 us -> 5.99 us  [give_back(): return lax.all_to_all(out, 'ep', 0, 0).reshape(ep_size * count * cap, model)]
    gather x14 -> x0, local copies, waits for them, and re-layouts: 65.6 us -> none  [the longest x2 18.1 us: device_step(): picked = jnp.take(back_rows, slot_of, axis=0)]
    psum x2 -> x1, waiting for transfers between devices: 81.3 us -> 20.1 us  [device_step(): lax.psum(jnp.einsum('td,te->de', x, d_logits, preferred_element_type=F32)...]
  transfers between devices with their start and end apart: 13 -> 21, of which waited for: 9 -> 10; matrix products, arithmetic and copies ran while one was open for 19% -> 29% of each run, Pallas kernels for 0% -> 19%
where the time goes in v1:
time: 608 us; the launch traced here: 601 us
  waiting for transfers between devices  232 us (38%)
  Pallas kernels  112 us (18%)
  matrix products  107 us (18%)
  local copies, waits for them, and re-layouts  75.4 us (12%)
  starting transfers between devices  36.3 us (6%)
  between operations  15.3 us (3%)
  blocking collectives  12.1 us (2%)
  other arithmetic  11.1 us (2%)
    dot_general x41, matrix products, dot(): return lax.dot_general(a, b, dims, preferred_element_type=F32)  103 us
    ppermute x3, waiting for transfers between devices, device_step(): fwd_parts.append((lax.ppermute(send, 'tp', swap), own))  76.9 us
    ppermute x3, waiting for transfers between devices, device_step(): bwd_parts = [(lax.ppermute(send, 'tp', swap), own) for send, own in bwd_out]  75.3 us
    pallas_call x1, Pallas kernels, expert_bwd(): pl.pallas_call(functools.partial(bwd_kernel, half, padded, starts), grid=...  70 us
    pallas_call x3, Pallas kernels, expert_fwd(): pl.pallas_call(functools.partial(fwd_kernel, half, padded), grid=(count,)...  41.6 us
    all_gather x1, waiting for transfers between devices, device_step(): x_all = lax.all_gather(x, ('ep', 'tp'), axis=0, tiled=True)  26.9 us
    ppermute x3, waiting for transfers between devices, other_half(): lax.ppermute(quarter, 'tp', swap)  25.7 us
    unnamed x167, local copies, waits for them, and re-layouts  25.4 us
  transfers between devices with their start and end apart: 21, of which 10 were waited for; matrix products, arithmetic and copies ran while one was open for 29% of the time, Pallas kernels for 19%

profile of v1, /device:TPU:0, one launch (start us, length us, event | category | flops | bytes accessed | tf_op | source)
XLA Modules:
  0.0 601.0 jit_solution(10724284820168288458)
XLA Ops:
  8.6 3.4 collective-permute-start.1
  12.0 9.1 %collective-permute-done.1 = bf16[384,512]{1,0:T(8,128)(2,1)S(1)} collective-permute-done((bf16[384,512]{1,0:T(8,128)(2,1)S(1)}, bf16[384,512]{1,0:T(8,128)(2,1)S(1)}, u32[]{:S(2)}, u32[]{:S(2)}) %collective-permute-start.1) | collective-permute-done | bytes 393248 | tf_op jit(solution)/shard_map/ppermute | solution.py:233
  24.8 8.5 %collective-permute-done = bf16[384,512]{1,0:T(8,128)(2,1)S(1)} collective-permute-done((bf16[384,512]{1,0:T(8,128)(2,1)S(1)}, bf16[384,512]{1,0:T(8,128)(2,1)S(1)}, u32[]{:S(2)}, u32[]{:S(2)}) %collective-permute-start) | collective-permute-done | bytes 393248 | tf_op jit(solution)/shard_map/ppermute | solution.py:233
  36.6 8.1 %collective-permute-done.2 = bf16[128,1536]{1,0:T(8,128)(2,1)S(1)} collective-permute-done((bf16[128,1536]{1,0:T(8,128)(2,1)S(1)}, bf16[128,1536]{1,0:T(8,128)(2,1)S(1)}, u32[]{:S(2)}, u32[]{:S(2)}) %collective-permute-start.2) | collective-permute-done | bytes 393248 | tf_op jit(solution)/shard_map/ppermute | solution.py:233
  46.7 12.1 %all-gather = s32[8,192,6]{1,2,0:T(8,128)S(1)} all-gather(s32[1,192,6]{1,2,0:T(8,128)S(1)} %bitcast.156), channel_id=1, replica_groups=mesh['tp'=2,'ep'=4] {'ep','tp'}, dimensions={0}, use_global_device_ids=true | all-gather | bytes 41472 | tf_op jit(solution)/shard_map/all_gather | solution.py:203
  77.2 2.6 fusion.33
  81.8 2.2 fusion.29
  85.8 26.9 %all-gather.13.cloned.1.call-done.x_ref = bf16[1536,1536]{1,0:T(8,128)(2,1)} async-done(((bf16[192,1536]{1,0:T(8,128)(2,1)}), bf16[1536,1536]{1,0:T(8,128)(2,1)}) %all-gather.13.cloned.1.call-update) | async-done | bytes 4718608 | tf_op jit(solution)/shard_map/all_gather | solution.py:202
  112.7 2.3 copy-done.2
  115.1 22.5 %expert_fwd_6.1 = (f32[840,1536]{1,0:T(8,128)}, f32[840,1536]{1,0:T(8,128)}) custom-call(bf16[1536,1536]{1,0:T(8,128)(2,1)S(1)} %copy-done.2, s32[16,1,1536]{2,1,0:T(1,128)S(1)} %reshape.699.row_ref, bf16[16,1536,256]{2,1,0:T(8,128)(2,1)} %w1_ref.7, bf16[16,1536,256]{2,1,0:T(8,128)(2,1)} %w3_ref.7, bf16[16,256,1536]{2,1,0:T(8,128)(2,1)} %w2_ref.7), custom_call_target="tpu_custom_call" | custom-call | flops 12457082880 | bytes 38633472 | tf_op jit(solution)/shard_map/expert_fwd_6/pallas_call | solution.py:107
  138.8 11.2 %expert_fwd_2.1 = (f32[336,1536]{1,0:T(8,128)}, f32[336,1536]{1,0:T(8,128)S(1)}) custom-call(bf16[1536,1536]{1,0:T(8,128)(2,1)} %all-gather.13.cloned.1.call-done.x_ref, s32[16,1,1536]{2,1,0:T(1,128)S(1)} %reshape.699.row_ref, bf16[16,1536,256]{2,1,0:T(8,128)(2,1)} %w1_ref.7, bf16[16,1536,256]{2,1,0:T(8,128)(2,1)} %w3_ref.7, bf16[16,256,1536]{2,1,0:T(8,128)(2,1)} %w2_ref.7), custom_call_target="tpu_custom_call" | custom-call | flops 4982833152 | bytes 18284544 | tf_op jit(solution)/shard_map/expert_fwd_2/pallas_call | solution.py:107
  152.1 7.9 %expert_fwd_0.1 = (f32[168,1536]{1,0:T(8,128)}, f32[168,1536]{1,0:T(8,128)S(1)}) custom-call(bf16[1536,1536]{1,0:T(8,128)(2,1)} %all-gather.13.cloned.1.call-done.x_ref, s32[16,1,1536]{2,1,0:T(1,128)S(1)} %reshape.699.row_ref, bf16[16,1536,256]{2,1,0:T(8,128)(2,1)} %w1_ref.7, bf16[16,1536,256]{2,1,0:T(8,128)(2,1)} %w3_ref.7, bf16[16,256,1536]{2,1,0:T(8,128)(2,1)} %w2_ref.7), custom_call_target="tpu_custom_call" | custom-call | flops 2491416576 | bytes 11501568 | tf_op jit(solution)/shard_map/expert_fwd_0/pallas_call | solution.py:107
  163.5 70.0 %expert_bwd.1 = (f32[16,1536,256]{2,1,0:T(8,128)}, f32[16,1536,256]{2,1,0:T(8,128)}, f32[16,256,1536]{2,1,0:T(8,128)}, f32[840,1536]{1,0:T(8,128)}, f32[840,1536...) custom-call(bf16[1536,1536]{1,0:T(8,128)(2,1)} %all-gather.13.cloned.1.ca, ...), custom_call_target="tpu_custom_call" | custom-call | flops 44291850240 | bytes 139198464 | tf_op jit(solution)/shard_map/expert_bwd/pallas_call | solution.py:143
  235.6 6.6 %convolution_convert_fusion.3 = bf16[1536,512]{1,0:T(8,128)(2,1)} fusion(bf16[1536,1536]{1,0:T(8,128)(2,1)} %all-gather.13.cloned.1.call-done.x_ref, bf16[1536,512]{1,0:T(8,128)(2,1)S(1)} %copy-done), kind=kOutput, calls=%fused_computation.24 | convolution fusion | flops 2416705536 | bytes 7864320 | tf_op jit(solution)/shard_map/dot_general | solution.py:22
  242.2 3.9 convolution_convert_fusion.4
  246.0 76.9 %collective-permute-done.3 = f32[168,1536]{1,0:T(8,128)} collective-permute-done((f32[168,1536]{1,0:T(8,128)}, f32[168,1536]{1,0:T(8,128)}, u32[]{:S(2)}, u32[]{:S(2)}) %collective-permute-start.3) | collective-permute-done | bytes 1032224 | tf_op jit(solution)/shard_map/ppermute | solution.py:220
  325.8 3.7 all-to-all-start
  329.6 6.1 %convolution_convert_fusion.2 = bf16[1536,512]{1,0:T(8,128)(2,1)} fusion(bf16[1536,1536]{1,0:T(8,128)(2,1)} %all-gather.13.cloned.1.call-done.x_ref, bf16[1536,512]{1,0:T(8,128)(2,1)S(1)} %copy-done.15), kind=kOutput, calls=%fused_computation.23 | convolution fusion | flops 2416705536 | bytes 7864320 | tf_op jit(solution)/shard_map/dot_general | solution.py:22
  335.7 53.6 %collective-permute-done.8 = f32[168,1536]{1,0:T(8,128)} collective-permute-done((f32[168,1536]{1,0:T(8,128)}, f32[168,1536]{1,0:T(8,128)}, u32[]{:S(2)}, u32[]{:S(2)}) %collective-permute-start.8) | collective-permute-done | bytes 1032224 | tf_op jit(solution)/shard_map/ppermute | solution.py:228
  391.8 3.5 all-to-all-start.5
  395.3 8.9 %convolution_bitcast_fusion.1 = f32[1536,512]{0,1:T(8,128)} fusion(bf16[1536,1536]{1,0:T(8,128)(2,1)} %all-gather.13.cloned.1.call-done.x_ref, bf16[1536,512]{1,0:T(8,128)(2,1)} %convolution_convert_fusion.3, bf16[1536,512]{1,0:T(8,128)(2,1)} %convolution_convert_fusion.4, bf16[1536,512]{1,0:T(8,128)(2,1)} %convolution_convert_fusion.2), kind=kOutput, calls=%fused_computation.11 | convolution fusion | flops 2426929152 | bytes 12582912 | tf_op jit(solution)/shard_map/dot_general | solution.py:22
  404.3 2.4 convolution_convert_fusion.6
  408.6 3.5 all-to-all-start.1
  412.2 7.4 %convolution_bitcast_fusion = f32[1536,512]{0,1:T(8,128)} fusion(bf16[1536,1536]{1,0:T(8,128)(2,1)} %all-gather.13.cloned.1.call-done.x_ref, bf16[1536,512]{1,0:T(8,128)(2,1)S(1)} %copy-done.77, bf16[1536,512]{1,0:T(8,128)(2,1)} %convolution_convert_fusion.2), kind=kOutput, calls=%fused_computation.10 | convolution fusion | flops 2422996992 | bytes 11010048 | tf_op jit(solution)/shard_map/dot_general | solution.py:22
  419.5 2.4 convolution_convert_fusion.5
  423.0 3.7 all-to-all-done.1
  426.7 3.5 all-to-all-start.4
  430.2 8.3 %convolution_convert_fusion.1 = bf16[840,1536]{1,0:T(8,128)(2,1)} fusion(f32[840,1536]{1,0:T(8,128)} %collective-permute-done.5, f32[840,1536]{1,0:T(8,128)} %get-tuple-element.29, s32[840]{0:T(1024)S(1)} %fusion.79), kind=kOutput, calls=%fused_computation.9 | convolution fusion | flops 2172179456 | bytes 12905760 | tf_op jit(solution)/shard_map/dot_general | solution.py:22
  438.5 3.9 reshape.704
  442.4 2.3 all-to-all-done.4
  445.7 5.0 all-to-all-start.2
  450.7 7.7 %fusion.17 = f32[512,1536]{1,0:T(8,128)} fusion(bf16[1536,1536]{1,0:T(8,128)(2,1)} %all-gather.15.cloned.1.call-done.dy_ref, bf16[1536,512]{1,0:T(8,128)(2,1)} %convolution_convert_fusion.3, bf16[1536,512]{1,0:T(8,128)(2,1)} %convolution_convert_fusion.2), kind=kOutput, calls=%fused_computation.52 | convolution fusion | flops 2422996992 | bytes 11010048 | tf_op jit(solution)/shard_map/dot_general | solution.py:22
  458.4 3.5 copy.53
  461.9 3.6 copy.54
  468.0 2.3 fusion.34
  478.0 21.7 %collective-permute-done.6 = f32[840,1536]{1,0:T(8,128)} collective-permute-done((f32[840,1536]{1,0:T(8,128)}, f32[840,1536]{1,0:T(8,128)}, u32[]{:S(2)}, u32[]{:S(2)}) %collective-permute-start.6) | collective-permute-done | bytes 5160992 | tf_op jit(solution)/shard_map/ppermute | solution.py:228
  499.6 8.3 %convolution_convert_fusion = bf16[840,1536]{1,0:T(8,128)(2,1)} fusion(f32[840,1536]{1,0:T(8,128)} %collective-permute-done.6, f32[840,1536]{1,0:T(8,128)} %get-tuple-element.31, s32[840]{0:T(1024)S(1)} %copy-done.75), kind=kOutput, calls=%fused_computation.8 | convolution fusion | flops 2172179456 | bytes 12905760 | tf_op jit(solution)/shard_map/dot_general | solution.py:22
  508.0 4.0 reshape.712
  512.0 4.5 all-to-all-start.3
  516.7 3.9 reshape.705
  520.6 3.8 fusion.24
  524.4 2.3 copy.52
  526.8 2.3 reshape.711
  537.7 2.3 fusion.40
  540.0 2.1 convert_element_type.296
  559.9 4.0 reshape.713
  563.9 3.4 fusion.12
  572.1 20.1 %all-reduce.2.cloned.1.call-done = f32[1536,64]{0,1:T(8,128)} async-done(((f32[1536,64]{0,1:T(8,128)}), f32[1536,64]{0,1:T(8,128)}) %all-reduce.2.cloned.1.call-update) | async-done | bytes 393232 | tf_op jit(solution)/shard_map/psum | solution.py:293
  (298 shorter events, 93.4 us)
Async XLA Ops:
  7.2 70.0 %all-gather.9.cloned.1.call-start = ((), (), s32[]{:S(2)}) async-start(), calls=%async_computation.7 | async-start | bytes 1966080 | tf_op jit(solution)/shard_map/all_gather | solution.py:233
  8.6 12.5 %collective-permute-start.1 = (bf16[384,512]{1,0:T(8,128)(2,1)S(1)}, bf16[384,512]{1,0:T(8,128)(2,1)S(1)}, u32[]{:S(2)}, u32[]{:S(2)}) collective-permute-start(bf16[384,512]{1,0:T(8,128)(2,1)S(1)} %constant_dynamic-slice_fusion.1), channel_id=1, source_target_pairs={{0,4},{4,0},{1,5},{5,1},{2,6},{6,2},{3,7},{7,3}} | collective-permute-start | bytes 1179656 | tf_op jit(solution)/shard_map/ppermute | solution.py:233
  21.9 58.0 %all-gather.7.cloned.1.call-start = ((), (), s32[]{:S(2)}) async-start(), calls=%async_computation.6 | async-start | bytes 1966080 | tf_op jit(solution)/shard_map/all_gather | solution.py:233
  23.0 23.7 %copy-start.67 = (s32[192,6]{0,1:T(8,128)S(1)}, s32[192,6]{0,1:T(8,128)}, u32[]{:S(2)}) copy-start(s32[192,6]{0,1:T(8,128)} %param.19) | copy-start | bytes 13828
  23.0 10.3 %collective-permute-start = (bf16[384,512]{1,0:T(8,128)(2,1)S(1)}, bf16[384,512]{1,0:T(8,128)(2,1)S(1)}, u32[]{:S(2)}, u32[]{:S(2)}) collective-permute-start(bf16[384,512]{1,0:T(8,128)(2,1)S(1)} %constant_dynamic-slice_fusion.2), channel_id=1, source_target_pairs={{0,4},{4,0},{1,5},{5,1},{2,6},{6,2},{3,7},{7,3}} | collective-permute-start | bytes 1179656 | tf_op jit(solution)/shard_map/ppermute | solution.py:233
  34.1 47.7 %all-gather.11.cloned.1.call-start = ((), (), s32[]{:S(2)}) async-start(), calls=%async_computation.8 | async-start | bytes 1966080 | tf_op jit(solution)/shard_map/all_gather | solution.py:233
  35.1 9.6 %collective-permute-start.2 = (bf16[128,1536]{1,0:T(8,128)(2,1)S(1)}, bf16[128,1536]{1,0:T(8,128)(2,1)S(1)}, u32[]{:S(2)}, u32[]{:S(2)}) collective-permute-start(bf16[128,1536]{1,0:T(8,128)(2,1)S(1)} %constant_dynamic-slice_fusion), channel_id=1, source_target_pairs={{0,4},{4,0},{1,5},{5,1},{2,6},{6,2},{3,7},{7,3}} | collective-permute-start | bytes 1179656 | tf_op jit(solution)/shard_map/ppermute | solution.py:233
  45.5 67.3 %all-gather.13.cloned.1.call-start = ((), (), s32[]{:S(2)}) async-start(), calls=%async_computation.9 | async-start | bytes 5308416 | tf_op jit(solution)/shard_map/all_gather | solution.py:202
  46.0 117.4 %all-gather.15.cloned.1.call-start = ((), (), s32[]{:S(2)}) async-start(), calls=%async_computation.10 | async-start | bytes 5308416 | tf_op jit(solution)/shard_map/all_gather | solution.py:204
  60.4 91.7 %copy-start.5 = (s32[16,1,1536]{2,1,0:T(1,128)}, s32[16,1,1536]{2,1,0:T(1,128)S(1)}, u32[]{:S(2)}) copy-start(s32[16,1,1536]{2,1,0:T(1,128)S(1)} %reshape.699.row_ref) | copy-start | bytes 294916
  61.8 7.8 %copy-start.7 = (bf16[192,1536]{1,0:T(8,128)(2,1)S(1)}, bf16[192,1536]{1,0:T(8,128)(2,1)}, u32[]{:S(2)}) copy-start(bf16[192,1536]{1,0:T(8,128)(2,1)} %param.10) | copy-start | bytes 1769476
  61.8 7.8 %copy-start.33 = (bf16[1536,64]{0,1:T(8,128)(2,1)S(1)}, bf16[1536,64]{0,1:T(8,128)(2,1)}, u32[]{:S(2)}) copy-start(bf16[1536,64]{0,1:T(8,128)(2,1)} %param.12) | copy-start | bytes 589828
  64.9 6.2 %copy-start.61 = (s32[4,4,21]{2,1,0:T(4,128)}, s32[4,4,21]{2,1,0:T(4,128)S(1)}, u32[]{:S(2)}) copy-start(s32[4,4,21]{2,1,0:T(4,128)S(1)} %add_select_fusion.1) | copy-start | bytes 4036
  65.8 4.7 copy-start.55
  69.0 361.2 %copy-start.74 = (s32[840]{0:T(1024)}, s32[840]{0:T(1024)S(1)}, u32[]{:S(2)}) copy-start(s32[840]{0:T(1024)S(1)} %fusion.79) | copy-start | bytes 10084
  137.5 292.7 %collective-permute-start.5 = (f32[840,1536]{1,0:T(8,128)}, f32[840,1536]{1,0:T(8,128)}, u32[]{:S(2)}, u32[]{:S(2)}) collective-permute-start(f32[840,1536]{1,0:T(8,128)} %get-tuple-element.28), channel_id=1, source_target_pairs={{0,4},{4,0},{1,5},{5,1},{2,6},{6,2},{3,7},{7,3}} | collective-permute-start | bytes 15482888 | tf_op jit(solution)/shard_map/ppermute | solution.py:220
  151.3 9.8 %slice-start = ((s8[4718592]{0:T(1024)(128)(4,1)}), s8[4194304]{0:T(1024)(128)(4,1)S(1)}, s32[]{:S(2)}) async-start(s8[4718592]{0:T(1024)(128)(4,1)} %bitcast.148), calls=%async_computation.12 | async-start | bytes 8388608
  151.3 9.8 %slice-start.1 = ((s8[4718592]{0:T(1024)(128)(4,1)}), s8[524288]{0:T(1024)(128)(4,1)S(1)}, s32[]{:S(2)}) async-start(s8[4718592]{0:T(1024)(128)(4,1)} %bitcast.148), calls=%async_computation.13 | async-start | bytes 1048576
  151.3 252.9 %collective-permute-start.4 = (f32[336,1536]{1,0:T(8,128)}, f32[336,1536]{1,0:T(8,128)}, u32[]{:S(2)}, u32[]{:S(2)}) collective-permute-start(f32[336,1536]{1,0:T(8,128)} %get-tuple-element.26), channel_id=1, source_target_pairs={{0,4},{4,0},{1,5},{5,1},{2,6},{6,2},{3,7},{7,3}} | collective-permute-start | bytes 6193160 | tf_op jit(solution)/shard_map/ppermute | solution.py:220
  160.0 162.9 %collective-permute-start.3 = (f32[168,1536]{1,0:T(8,128)}, f32[168,1536]{1,0:T(8,128)}, u32[]{:S(2)}, u32[]{:S(2)}) collective-permute-start(f32[168,1536]{1,0:T(8,128)} %get-tuple-element.24), channel_id=1, source_target_pairs={{0,4},{4,0},{1,5},{5,1},{2,6},{6,2},{3,7},{7,3}} | collective-permute-start | bytes 3096584 | tf_op jit(solution)/shard_map/ppermute | solution.py:220
  233.5 186.0 %collective-permute-start.7 = (f32[336,1536]{1,0:T(8,128)}, f32[336,1536]{1,0:T(8,128)}, u32[]{:S(2)}, u32[]{:S(2)}) collective-permute-start(f32[336,1536]{1,0:T(8,128)} %get-tuple-element.32), channel_id=1, source_target_pairs={{0,4},{4,0},{1,5},{5,1},{2,6},{6,2},{3,7},{7,3}} | collective-permute-start | bytes 6193160 | tf_op jit(solution)/shard_map/ppermute | solution.py:228
  234.4 7.7 %slice-start.2 = ((s8[4718592]{0:T(1024)(128)(4,1)}), s8[4194304]{0:T(1024)(128)(4,1)S(1)}, s32[]{:S(2)}) async-start(s8[4718592]{0:T(1024)(128)(4,1)} %bitcast.157), calls=%async_computation.14 | async-start | bytes 8388608
  234.4 7.7 %copy-start.13 = (bf16[512,1536]{1,0:T(8,128)(2,1)S(1)}, bf16[512,1536]{1,0:T(8,128)(2,1)}, u32[]{:S(2)}) copy-start(bf16[512,1536]{1,0:T(8,128)(2,1)} %param.18) | copy-start | bytes 4718596
  234.4 7.7 %slice-start.3 = ((s8[4718592]{0:T(1024)(128)(4,1)}), s8[524288]{0:T(1024)(128)(4,1)S(1)}, s32[]{:S(2)}) async-start(s8[4718592]{0:T(1024)(128)(4,1)} %bitcast.157), calls=%async_computation.15 | async-start | bytes 1048576
  234.4 154.8 %collective-permute-start.8 = (f32[168,1536]{1,0:T(8,128)}, f32[168,1536]{1,0:T(8,128)}, u32[]{:S(2)}, u32[]{:S(2)}) collective-permute-start(f32[168,1536]{1,0:T(8,128)} %get-tuple-element.34), channel_id=1, source_target_pairs={{0,4},{4,0},{1,5},{5,1},{2,6},{6,2},{3,7},{7,3}} | collective-permute-start | bytes 3096584 | tf_op jit(solution)/shard_map/ppermute | solution.py:228
  322.9 176.7 %collective-permute-start.6 = (f32[840,1536]{1,0:T(8,128)}, f32[840,1536]{1,0:T(8,128)}, u32[]{:S(2)}, u32[]{:S(2)}) collective-permute-start(f32[840,1536]{1,0:T(8,128)} %get-tuple-element.30), channel_id=1, source_target_pairs={{0,4},{4,0},{1,5},{5,1},{2,6},{6,2},{3,7},{7,3}} | collective-permute-start | bytes 15482888 | tf_op jit(solution)/shard_map/ppermute | solution.py:228
  324.9 4.7 copy-start.15
  325.8 66.0 %all-to-all-start = ((bf16[4,42,1536]{2,1,0:T(8,128)(2,1)}), bf16[4,42,1536]{2,1,0:T(8,128)(2,1)S(1)}, u32[]{:S(2)}, u32[]{:S(2)}) async-start(bf16[4,42,1536]{2,1,0:T(8,128)(2,1)} %reshape.700), calls=%async_computation | async-start | bytes 1179648 | tf_op jit(solution)/shard_map/all_to_all | solution.py:262
  329.5 59.8 %copy-start.37 = (f32[168,1536]{1,0:T(8,128)S(1)}, f32[168,1536]{1,0:T(8,128)}, u32[]{:S(2)}) copy-start(f32[168,1536]{1,0:T(8,128)} %get-tuple-element.35) | copy-start | bytes 3096580
  391.8 12.4 %copy-start.27 = (bf16[4,42,1536]{2,1,0:T(8,128)(2,1)}, bf16[4,42,1536]{2,1,0:T(8,128)(2,1)S(1)}, u32[]{:S(2)}) copy-start(bf16[4,42,1536]{2,1,0:T(8,128)(2,1)S(1)} %all-to-all-done) | copy-start | bytes 1548292
  391.8 16.0 %all-to-all-start.5 = ((bf16[4,42,1536]{2,1,0:T(8,128)(2,1)}), bf16[4,42,1536]{2,1,0:T(8,128)(2,1)S(1)}, u32[]{:S(2)}, u32[]{:S(2)}) async-start(bf16[4,42,1536]{2,1,0:T(8,128)(2,1)} %reshape.716), calls=%async_computation.5 | async-start | bytes 1179648 | tf_op jit(solution)/shard_map/all_to_all | solution.py:262
  395.3 9.0 %copy-start.4 = (f32[336,1536]{1,0:T(8,128)S(1)}, f32[336,1536]{1,0:T(8,128)}, u32[]{:S(2)}) copy-start(f32[336,1536]{1,0:T(8,128)} %copy-done.3) | copy-start | bytes 6193156
  407.8 4.4 copy-start.77
  408.6 18.1 %all-to-all-start.1 = ((bf16[4,84,1536]{2,1,0:T(8,128)(2,1)}), bf16[4,84,1536]{2,1,0:T(8,128)(2,1)S(1)}, u32[]{:S(2)}, u32[]{:S(2)}) async-start(bf16[4,84,1536]{2,1,0:T(8,128)(2,1)} %reshape.702), calls=%async_computation.1 | async-start | bytes 2162688 | tf_op jit(solution)/shard_map/all_to_all | solution.py:262
  412.1 7.4 %copy-start.31 = (f32[336,1536]{1,0:T(8,128)S(1)}, f32[336,1536]{1,0:T(8,128)}, u32[]{:S(2)}) copy-start(f32[336,1536]{1,0:T(8,128)} %get-tuple-element.33) | copy-start | bytes 6193156
  426.7 18.1 %all-to-all-start.4 = ((bf16[4,84,1536]{2,1,0:T(8,128)(2,1)}), bf16[4,84,1536]{2,1,0:T(8,128)(2,1)S(1)}, u32[]{:S(2)}, u32[]{:S(2)}) async-start(bf16[4,84,1536]{2,1,0:T(8,128)(2,1)} %reshape.714), calls=%async_computation.4 | async-start | bytes 2162688 | tf_op jit(solution)/shard_map/all_to_all | solution.py:262
  445.7 66.3 %all-to-all-start.2 = ((bf16[4,210,1536]{2,1,0:T(8,128)(2,1)}), bf16[4,210,1536]{2,1,0:T(8,128)(2,1)}, u32[]{:S(2)}, u32[]{:S(2)}) async-start(bf16[4,210,1536]{2,1,0:T(8,128)(2,1)} %reshape.704), calls=%async_computation.2 | async-start | bytes 5308416 | tf_op jit(solution)/shard_map/all_to_all | solution.py:262
  468.0 7.0 %copy-start.23 = (bf16[4,84,1536]{2,1,0:T(8,128)(2,1)S(1)}, bf16[4,84,1536]{2,1,0:T(8,128)(2,1)}, u32[]{:S(2)}) copy-start(bf16[4,84,1536]{2,1,0:T(8,128)(2,1)} %copy-done.22) | copy-start | bytes 3096580
  476.2 23.5 %copy-start.75 = (s32[840]{0:T(1024)S(1)}, s32[840]{0:T(1024)}, u32[]{:S(2)}) copy-start(s32[840]{0:T(1024)} %copy-done.74) | copy-start | bytes 10084
  512.0 48.0 %all-to-all-start.3 = ((bf16[4,210,1536]{2,1,0:T(8,128)(2,1)}), bf16[4,210,1536]{2,1,0:T(8,128)(2,1)}, u32[]{:S(2)}, u32[]{:S(2)}) async-start(bf16[4,210,1536]{2,1,0:T(8,128)(2,1)} %reshape.712), calls=%async_computation.3 | async-start | bytes 5308416 | tf_op jit(solution)/shard_map/all_to_all | solution.py:262
  516.5 75.7 %all-reduce.2.cloned.1.call-start = ((), (), s32[]{:S(2)}) async-start(), calls=%async_computation.11 | async-start | bytes 786432 | tf_op jit(solution)/shard_map/psum | solution.py:293
  526.8 5.6 copy-start.64
  526.8 5.6 copy-start.66
  530.4 4.9 copy-start.59
  530.4 4.9 copy-start.62
  540.0 6.1 %copy-start.73 = (f32[192]{0:T(256)S(1)}, f32[192]{0:T(256)}, u32[]{:S(2)}) copy-start(f32[192]{0:T(256)} %get-tuple-element.75) | copy-start | bytes 2308
  540.0 7.6 %copy-start.8 = (bf16[192,1536]{1,0:T(8,128)(2,1)S(1)}, bf16[192,1536]{1,0:T(8,128)(2,1)}, u32[]{:S(2)}) copy-start(bf16[192,1536]{1,0:T(8,128)(2,1)} %param.10) | copy-start | bytes 1769476
  569.5 24.4 %copy-start.1 = (bf16[1536,512]{1,0:T(8,128)(2,1)S(1)}, bf16[1536,512]{1,0:T(8,128)(2,1)}, u32[]{:S(2)}) copy-start(bf16[1536,512]{1,0:T(8,128)(2,1)} %param.17) | copy-start | bytes 4718596
  (55 other events, 109.9 us)
Sparse Core Ops, SparseCore 0:
  22.0 17.8 all-gather.8
  42.0 17.1 all-gather.6
  61.3 16.7 all-gather.10
  79.8 32.9 all-gather.12
  114.4 38.5 all-gather.14
  548.7 43.4 all-reduce.1
